TPU v7x, 32 devices: a whole 2x2x4 slice. The times are simulated.
32 devices in a mesh: tile: 8 (over z, x), conv: 4 (over y, core).
Axes of the slice: x: 2, y: 2, z: 4, core: 2. Of those that a mesh axis runs over, the one named last changes fastest.
Arguments:
- field: float32 [256, 24576], P(None, ('tile', 'conv')), may hold values from -6 to 6
- interp: bfloat16 [32768, 384], P(('tile', 'conv')), may hold values from -0.1875 to 0.1875
- conv_blocks: bfloat16 [64, 3, 256, 256], P(('tile', 'conv')), may hold values from -0.21875 to 0.21875
- band_shift: int32 [64, 3], P(('tile', 'conv')), may hold values from 0 to 1
- owner: int32 [12288, 1], P(('tile', 'conv')), may hold values from 0 to 3; in each aligned block of 384 rows (0 to 383, 384 to 767, ...) at most 128 rows name the same one
- edge_index: int32 [64, 128], P(('tile', 'conv')), may hold values from 0 to 767, as said below
Outputs:
- correlated: float32 [256, 24576], P(None, ('tile', 'conv'))
Inputs may be any that keep to these rules, and one draw needn't show every extreme that they name: `edge_index`: row 2b lists the first 128 columns of domain b in some order, row 2b + 1 its last 128 columns in some order. Among the 384 points of one domain no owner is named more than 128 times, and in some domains one owner is named exactly 128 times.
All inputs are finite; a program needn't handle non-finite values.
Results may differ from a plain program's by a relative error of at most 0.0049.
Values may be sent and summed in bfloat16 or wider, within the bound.
A program may use at most 64 MiB of HBM per device.

v0:
```python
import jax
import jax.numpy as jnp
from jax import lax
from jax.sharding import PartitionSpec as P


def padded(cells, sides, width):
    for axis, dim in sides:
        count = lax.axis_size(axis)
        head = lax.slice_in_dim(cells, 0, width, axis=dim)
        tail = lax.slice_in_dim(cells, cells.shape[dim] - width, cells.shape[dim], axis=dim)
        cells = jnp.concatenate(
            [
                lax.ppermute(tail, axis, [(i, (i + 1) % count) for i in range(count)]),
                cells,
                lax.ppermute(head, axis, [((i + 1) % count, i) for i in range(count)]),
            ],
            axis=dim,
        )
    return cells


def contract_last(left_side, right_side):
    return lax.dot_general(
        left_side, right_side, (((1,), (1,)), ((), ())), preferred_element_type=jnp.float32
    )


def convolve(values, conv_blocks, band_shift):
    height = values.shape[0]
    owned_blocks = conv_blocks.shape[0]
    points = conv_blocks.shape[2]
    pieces = values.reshape(height, owned_blocks, points)
    source = (jnp.arange(owned_blocks, dtype=jnp.int32)[:, None] + band_shift) % owned_blocks
    select = (
        source[:, :, None] == jnp.arange(owned_blocks, dtype=jnp.int32)[None, None, :]
    ).astype(jnp.bfloat16)
    picked = jnp.einsum("rsp,jbs->rjbp", pieces, select, preferred_element_type=jnp.float32).astype(
        jnp.bfloat16
    )
    forward = jnp.einsum(
        "rjbp,jbpq->rjq", picked, conv_blocks, preferred_element_type=jnp.float32
    ).astype(jnp.bfloat16)
    backward = jnp.einsum(
        "rjq,jbpq->rjbp", forward, conv_blocks, preferred_element_type=jnp.float32
    )
    adjoint = jnp.einsum(
        "rjbp,jbs->rsp", backward, select.astype(jnp.float32), precision=lax.Precision.HIGHEST
    )
    return adjoint.reshape(height, owned_blocks * points).astype(jnp.bfloat16)


def on_device(field, interp, conv_blocks, band_shift, owner, edge_index):
    columns = field.shape[1]
    rim_width = edge_index.shape[1]
    groups = lax.axis_size("conv")
    slot_count = conv_blocks.shape[0] * conv_blocks.shape[2]
    capacity = slot_count // groups
    rounded = field.astype(jnp.bfloat16)
    left_list = edge_index[0]
    right_list = edge_index[1]
    rim_values = jnp.concatenate(
        [jnp.take(rounded, left_list, axis=1), jnp.take(rounded, right_list, axis=1)], axis=1
    )
    widened = padded(rim_values, ((("tile", "conv"), 1),), rim_width)
    from_left = widened[:, :rim_width]
    from_right = widened[:, 3 * rim_width :]
    extended = jnp.concatenate([from_left, rounded, from_right], axis=1)
    subgrid = jnp.dot(extended, interp, preferred_element_type=jnp.float32)
    subgrid = subgrid.astype(jnp.bfloat16)
    owners = owner[:, 0]
    choose = (owners[:, None] == jnp.arange(groups, dtype=jnp.int32)[None, :]).astype(jnp.int32)
    before = jnp.cumsum(choose, axis=0) - choose
    position = jnp.sum(before * choose, axis=1)
    slot_index = owners * capacity + position
    placement = (slot_index[:, None] == jnp.arange(slot_count, dtype=jnp.int32)[None, :]).astype(
        jnp.bfloat16
    )
    outgoing = jnp.dot(subgrid, placement, preferred_element_type=jnp.float32).astype(jnp.bfloat16)
    incoming = lax.all_to_all(
        convolve(
            lax.all_to_all(outgoing, "conv", split_axis=1, concat_axis=1, tiled=True),
            conv_blocks,
            band_shift,
        ),
        "conv",
        split_axis=1,
        concat_axis=1,
        tiled=True,
    )
    returned = contract_last(incoming, placement).astype(jnp.bfloat16)
    partial_value = contract_last(returned, interp)
    left_part = partial_value[:, :rim_width]
    right_part = partial_value[:, rim_width + columns :]
    edge_sums = padded(
        jnp.concatenate([left_part, right_part], axis=1).astype(jnp.bfloat16),
        ((("tile", "conv"), 1),),
        rim_width,
    ).astype(jnp.float32)
    interior_part = partial_value[:, rim_width : rim_width + columns]
    result = interior_part.at[:, left_list].add(edge_sums[:, :rim_width])
    result = result.at[:, right_list].add(edge_sums[:, 3 * rim_width :])
    return result


def solution(mesh):
    return jax.shard_map(
        on_device,
        mesh=mesh,
        in_specs=(
            P(None, ("tile", "conv")),
            P(("tile", "conv"), None),
            P(("tile", "conv"), None, None, None),
            P(("tile", "conv"), None),
            P(("tile", "conv"), None),
            P(("tile", "conv"), None),
        ),
        out_specs=P(None, ("tile", "conv")),
        check_vma=False,
    )
```

profile of v0, /device:TPU:0, one launch (start us, length us, event | category | flops | bytes accessed | tf_op | source)
XLA Modules:
  0.0 51.1 jit_solution(18035988229664410516)
XLA Ops:
  0.0 0.0 copy-start
  0.0 0.0 copy-start.1
  0.0 0.8 %compare_and_fusion.1 = (pred[128]{0:T(512)(128)(4,1)S(1)}, s32[128]{0:T(128)S(1)}, pred[128]{0:T(512)(128)(4,1)S(1)}, s32[128]{0:T(128)S(1)}) fusion(s32[2,128]{1,0:T(2,128)} %param.13), kind=kLoop, calls=%fused_computation.58 | loop fusion | flops 1536 | bytes 2304 | tf_op jit(solution)/shard_map/jit(_take)/and | solution.py:63
  0.8 1.3 %copy.27 = bf16[256,768]{0,1:T(8,128)(2,1)S(1)} copy(f32[256,768]{1,0:T(8,128)} %param.8) | data formatting | bytes 1179648 | tf_op args[0]
  2.1 0.8 %gather_fusion = bf16[128,256]{1,0:T(8,128)(2,1)S(1)} fusion(bf16[256,768]{0,1:T(8,128)(2,1)S(1)} %copy.27, s32[1024]{0:T(1024)S(1)} %pad_clamp_fusion.1), kind=kCustom, calls=%fused_computation.clone | custom fusion | bytes 131584 | tf_op jit(solution)/shard_map/jit(_take)/gather | solution.py:63
  3.0 0.1 select_bitcast_fusion.1
  3.1 0.5 %collective-permute-start = (bf16[256,128]{0,1:T(8,128)(2,1)S(1)}, bf16[256,128]{0,1:T(8,128)(2,1)S(1)}, u32[]{:S(2)}, u32[]{:S(2)}) collective-permute-start(bf16[256,128]{0,1:T(8,128)(2,1)S(1)} %select_bitcast_fusion.1), channel_id=1, source_target_pairs={{0,1},{1,2},{2,3},{3,4},{4,5},{5,6},{6,7},{7,8},{8,9},{9,10},{10,1... | collective-permute-start | bytes 196616 | tf_op jit(solution)/shard_map/ppermute | solution.py:14
  3.6 0.8 %gather_fusion.1 = bf16[128,256]{1,0:T(8,128)(2,1)S(1)} fusion(bf16[256,768]{0,1:T(8,128)(2,1)S(1)} %copy.27, s32[1024]{0:T(1024)S(1)} %pad_clamp_fusion), kind=kCustom, calls=%fused_computation.1.clone | custom fusion | bytes 131584 | tf_op jit(solution)/shard_map/jit(_take)/gather | solution.py:63
  4.5 0.1 select_bitcast_fusion
  4.5 6.0 %collective-permute-start.1 = (bf16[256,128]{0,1:T(8,128)(2,1)S(1)}, bf16[256,128]{0,1:T(8,128)(2,1)S(1)}, u32[]{:S(2)}, u32[]{:S(2)}) collective-permute-start(bf16[256,128]{0,1:T(8,128)(2,1)S(1)} %select_bitcast_fusion), channel_id=1, source_target_pairs={{1,0},{2,1},{3,2},{4,3},{5,4},{6,5},{7,6},{8,7},{9,8},{10,9},{11,1... | collective-permute-start | bytes 196616 | tf_op jit(solution)/shard_map/ppermute | solution.py:16
  10.5 0.0 copy-done.1
  10.6 1.2 %reduce-window.6 = s32[4,3,128]{2,1,0:T(4,128)S(1)} reduce-window(s32[4,3,128]{2,1,0:T(4,128)S(1)} %fusion.32, s32[]{:T(128)} %constant.30.clone.1), window={size=1x1x128 pad=0_0x0_0x127_0}, to_apply=%region_0.0 | reduce-window | flops 195072 | bytes 12292 | tf_op jit(solution)/shard_map/reduce-window
  11.8 0.2 slice_reduce_fusion
  12.0 0.2 reduce-window.9
  12.2 0.1 add_bitcast_fusion
  12.3 0.0 copy-start.3
  12.3 0.0 collective-permute-done
  12.3 0.1 collective-permute-done.1
  12.4 0.0 copy-done
  12.4 0.7 %fusion.10 = bf16[32,4,8,128]{3,2,1,0:T(8,128)(2,1)S(1)} fusion(bf16[1024,384]{1,0:T(8,128)(2,1)S(1)} %copy-done, bf16[256,128]{0,1:T(8,128)(2,1)S(1)} %collective-permute-done.1, bf16[256,768]{0,1:T(8,128)(2,1)S(1)} %copy.27, bf16[256,128]{0,1:T(8,128)(2,1)S(1)} %collective-permute-done, s32[384]{0:T(512)S(1)} %add_reduce_fusion), kind=kOutput, calls=%fused_computation.16 | convolution fusion | flops 303988736 | bytes 1574400 | tf_op jit(solution)/shard_map/dot_general | solution.py:79
  13.1 0.7 %copy.58 = bf16[32,4,8,128]{3,2,0,1:T(8,128)(2,1)} copy(bf16[32,4,8,128]{3,2,1,0:T(8,128)(2,1)S(1)} %fusion.10) | data formatting | bytes 524288 | tf_op jit(solution)/shard_map/all_to_all | solution.py:82
  13.9 3.4 %all-to-all-start = ((bf16[256,4,128]{2,0,1:T(8,128)(2,1)}), bf16[256,4,128]{2,0,1:T(8,128)(2,1)S(1)}, u32[]{:S(2)}, u32[]{:S(2)}) async-start(bf16[256,4,128]{2,0,1:T(8,128)(2,1)} %bitcast.89), calls=%async_computation | async-start | bytes 524288 | tf_op jit(solution)/shard_map/all_to_all | solution.py:82
  17.3 0.0 copy-done.3
  17.3 5.9 %all-to-all-done = bf16[256,4,128]{2,0,1:T(8,128)(2,1)S(1)} async-done(((bf16[256,4,128]{2,0,1:T(8,128)(2,1)}), bf16[256,4,128]{2,0,1:T(8,128)(2,1)S(1)}, u32[]{:S(2)}, u32[]{:S(2)}) %all-to-all-start) | async-done | bytes 262176 | tf_op jit(solution)/shard_map/all_to_all | solution.py:82
  23.3 0.2 copy.29
  23.5 0.2 reshape.131
  23.7 1.0 %fusion.2 = bf16[256,2,3,256]{3,2,0,1:T(4,128)(2,1)S(1)} fusion(bf16[256,2,256,1]{2,1,0,3:T(2,128)(2,1)S(1)} %reshape.131, s32[2,3]{1,0:T(2,128)S(1)} %and_select_fusion), kind=kOutput, calls=%fused_computation.8 | convolution fusion | flops 1966092 | bytes 1048600 | tf_op jit(solution)/shard_map/rsp,jbs->rjbp/dot_general | solution.py:38
  24.7 2.0 %convolution_bitcast_fusion = f32[256,2,3,256]{3,0,2,1:T(8,128)S(1)} fusion(bf16[2,3,256,256]{3,2,1,0:T(8,128)(2,1)} %param.10, bf16[256,2,3,256]{3,2,0,1:T(4,128)(2,1)S(1)} %fusion.2), kind=kOutput, calls=%fused_computation.6 | convolution fusion | flops 402784256 | bytes 3145728 | tf_op jit(solution)/shard_map/rjq,jbpq->rjbp/dot_general | solution.py:44
  26.7 2.9 %fusion.11 = bf16[256,2,256]{2,1,0:T(2,128)(2,1)S(1)} fusion(f32[256,2,3,256]{3,0,2,1:T(8,128)S(1)} %convolution_bitcast_fusion, s32[2,3]{1,0:T(2,128)S(1)} %and_select_fusion), kind=kOutput, calls=%fused_computation.17 | convolution fusion | flops 9568268 | bytes 1835032 | tf_op jit(solution)/shard_map/rjbp,jbs->rsp/dot_general | solution.py:47
  29.6 0.2 convert_element_type.59
  29.9 8.4 %all_to_all.18 = bf16[256,4,128]{2,0,1:T(8,128)(2,1)S(1)} all-to-all(bf16[256,4,128]{2,0,1:T(8,128)(2,1)S(1)} %copy.32), channel_id=1, replica_groups=mesh['tile'=8,'conv'=4] {'conv'}, dimensions={1} | all-to-all | bytes 524288 | tf_op jit(solution)/shard_map/all_to_all | solution.py:80
  38.3 0.1 copy.33
  38.4 0.0 copy-start.2
  38.4 0.8 %fusion.46 = (bf16[256,1024]{1,0:T(8,128)(2,1)S(1)}, f32[256,1024]{1,0:T(8,128)S(1)}) fusion(bf16[1024,384]{1,0:T(8,128)(2,1)S(1)} %copy-done, bf16[256,512]{0,1:T(8,128)(2,1)S(1)} %bitcast.91, s32[384]{0:T(512)S(1)} %add_reduce_fusion), kind=kOutput, calls=%fused_computation.68 | convolution fusion | flops 302546944 | bytes 2622976 | tf_op jit(solution)/shard_map/dot_general | solution.py:24
  39.2 0.1 collective-permute-start.2
  39.3 5.3 %collective-permute-start.3 = (bf16[256,128]{1,0:T(8,128)(2,1)S(1)}, bf16[256,128]{1,0:T(8,128)(2,1)S(1)}, u32[]{:S(2)}, u32[]{:S(2)}) collective-permute-start(bf16[256,128]{1,0:T(8,128)(2,1)S(1)} %get-tuple-element.11), channel_id=1, source_target_pairs={{1,0},{2,1},{3,2},{4,3},{5,4},{6,5},{7,6},{8,7},{9,8},{10,9},{11,1... | collective-permute-start | bytes 196616 | tf_op jit(solution)/shard_map/ppermute | solution.py:16
  44.6 0.0 copy-done.2
  44.6 0.1 slice.45
  44.7 0.3 copy.34
  45.0 1.6 %collective-permute-done.2 = bf16[256,128]{1,0:T(8,128)(2,1)S(1)} collective-permute-done((bf16[256,128]{1,0:T(8,128)(2,1)S(1)}, bf16[256,128]{1,0:T(8,128)(2,1)S(1)}, u32[]{:S(2)}, u32[]{:S(2)}) %collective-permute-start.2) | collective-permute-done | bytes 65568 | tf_op jit(solution)/shard_map/ppermute | solution.py:14
  46.6 0.0 collective-permute-done.3
  46.6 0.1 copy.35
  46.7 0.1 copy.36
  46.8 1.6 %scatter_fusion = f32[256,768]{0,1:T(8,128)S(1)} fusion(f32[256,768]{0,1:T(8,128)S(1)} %copy.34, s32[128]{0:T(128)S(1)} %get-tuple-element.15, f32[128,256]{1,0:T(8,128)S(1)} %copy.35), kind=kCustom, calls=%fused_computation.2 | custom fusion | flops 32768 | bytes 393728 | tf_op jit(solution)/shard_map/scatter-add | solution.py:101
  48.4 1.6 %scatter_fusion.1 = f32[256,768]{0,1:T(8,128)S(1)} fusion(f32[256,768]{0,1:T(8,128)S(1)} %scatter_fusion, s32[128]{0:T(128)S(1)} %get-tuple-element.14, f32[128,256]{1,0:T(8,128)S(1)} %copy.36), kind=kCustom, calls=%fused_computation.3 | custom fusion | flops 32768 | bytes 393728 | tf_op jit(solution)/shard_map/scatter-add | solution.py:102
  50.0 1.1 %copy.37 = f32[256,768]{1,0:T(8,128)} copy(f32[256,768]{0,1:T(8,128)S(1)} %scatter_fusion.1) | data formatting | bytes 1572864 | tf_op jit(solution)/shard_map/scatter-add | solution.py:102
  (11 shorter events, 0.2 us)
Async XLA Ops:
  0.0 12.4 %copy-start = (bf16[1024,384]{1,0:T(8,128)(2,1)S(1)}, bf16[1024,384]{1,0:T(8,128)(2,1)}, u32[]{:S(2)}) copy-start(bf16[1024,384]{1,0:T(8,128)(2,1)} %param.9) | copy-start | bytes 2359300
  0.0 10.5 %copy-start.1 = (s32[384,1]{0,1:T(1,128)S(1)}, s32[384,1]{0,1:T(1,128)}, u32[]{:S(2)}) copy-start(s32[384,1]{0,1:T(1,128)} %param.12) | copy-start | bytes 4612
  3.1 9.3 %collective-permute-start = (bf16[256,128]{0,1:T(8,128)(2,1)S(1)}, bf16[256,128]{0,1:T(8,128)(2,1)S(1)}, u32[]{:S(2)}, u32[]{:S(2)}) collective-permute-start(bf16[256,128]{0,1:T(8,128)(2,1)S(1)} %select_bitcast_fusion.1), channel_id=1, source_target_pairs={{0,1},{1,2},{2,3},{3,4},{4,5},{5,6},{6,7},{7,8},{8,9},{9,10},{10,1... | collective-permute-start | bytes 196616 | tf_op jit(solution)/shard_map/ppermute | solution.py:14
  4.5 7.9 %collective-permute-start.1 = (bf16[256,128]{0,1:T(8,128)(2,1)S(1)}, bf16[256,128]{0,1:T(8,128)(2,1)S(1)}, u32[]{:S(2)}, u32[]{:S(2)}) collective-permute-start(bf16[256,128]{0,1:T(8,128)(2,1)S(1)} %select_bitcast_fusion), channel_id=1, source_target_pairs={{1,0},{2,1},{3,2},{4,3},{5,4},{6,5},{7,6},{8,7},{9,8},{10,9},{11,1... | collective-permute-start | bytes 196616 | tf_op jit(solution)/shard_map/ppermute | solution.py:16
  12.3 5.0 %copy-start.3 = (s32[2,3]{1,0:T(2,128)S(1)}, s32[2,3]{1,0:T(2,128)}, u32[]{:S(2)}) copy-start(s32[2,3]{1,0:T(2,128)} %param.11) | copy-start | bytes 76
  13.9 9.4 %all-to-all-start = ((bf16[256,4,128]{2,0,1:T(8,128)(2,1)}), bf16[256,4,128]{2,0,1:T(8,128)(2,1)S(1)}, u32[]{:S(2)}, u32[]{:S(2)}) async-start(bf16[256,4,128]{2,0,1:T(8,128)(2,1)} %bitcast.89), calls=%async_computation | async-start | bytes 524288 | tf_op jit(solution)/shard_map/all_to_all | solution.py:82
  38.4 6.2 %copy-start.2 = (s32[2,128]{1,0:T(2,128)S(1)}, s32[2,128]{1,0:T(2,128)}, u32[]{:S(2)}) copy-start(s32[2,128]{1,0:T(2,128)} %param.13) | copy-start | bytes 3076
  39.2 7.3 %collective-permute-start.2 = (bf16[256,128]{1,0:T(8,128)(2,1)S(1)}, bf16[256,128]{1,0:T(8,128)(2,1)S(1)}, u32[]{:S(2)}, u32[]{:S(2)}) collective-permute-start(bf16[256,128]{1,0:T(8,128)(2,1)S(1)} %get-tuple-element.10), channel_id=1, source_target_pairs={{0,1},{1,2},{2,3},{3,4},{4,5},{5,6},{6,7},{7,8},{8,9},{9,10},{10,1... | collective-permute-start | bytes 196616 | tf_op jit(solution)/shard_map/ppermute | solution.py:14
  39.3 7.3 %collective-permute-start.3 = (bf16[256,128]{1,0:T(8,128)(2,1)S(1)}, bf16[256,128]{1,0:T(8,128)(2,1)S(1)}, u32[]{:S(2)}, u32[]{:S(2)}) collective-permute-start(bf16[256,128]{1,0:T(8,128)(2,1)S(1)} %get-tuple-element.11), channel_id=1, source_target_pairs={{1,0},{2,1},{3,2},{4,3},{5,4},{6,5},{7,6},{8,7},{9,8},{10,9},{11,1... | collective-permute-start | bytes 196616 | tf_op jit(solution)/shard_map/ppermute | solution.py:16
where the time goes:
time: 51.4 us; the launch traced here: 51.1 us
  starting transfers between devices  15.3 us (30%)
  blocking collectives  8.39 us (16%)
  waiting for transfers between devices  7.66 us (15%)
  matrix products  7.43 us (14%)
  local copies, waits for them, and re-layouts  6.38 us (12%)
  other arithmetic  5.73 us (11%)
    ppermute x2, starting transfers between devices, padded(): lax.ppermute(head, axis, [((i + 1) % count, i) for i in range(count)])  11.3 us
    all_to_all x1, blocking collectives, on_device(): lax.all_to_all(convolve(lax.all_to_all(outgoing, 'conv', split_axis=1, co...  8.39 us
    all_to_all x1, waiting for transfers between devices, on_device(): lax.all_to_all(outgoing, 'conv', split_axis=1, concat_axis=1, tiled=True)  5.95 us
    all_to_all x1, starting transfers between devices, on_device(): lax.all_to_all(outgoing, 'conv', split_axis=1, concat_axis=1, tiled=True)  3.41 us
    dot_general x1, matrix products, convolve(): jnp.einsum('rjbp,jbs->rsp', backward, select.astype(jnp.float32), precisi...  2.94 us
    dot_general x1, matrix products, convolve(): jnp.einsum('rjq,jbpq->rjbp', forward, conv_blocks, preferred_element_type...  2.02 us
    ppermute x2, waiting for transfers between devices, padded(): lax.ppermute(tail, axis, [(i, (i + 1) % count) for i in range(count)])  1.61 us
    scatter-add x1, other arithmetic, on_device(): result = interior_part.at[:, left_list].add(edge_sums[:, :rim_width])  1.59 us
  transfers between devices with their start and end apart: 5, of which 3 were waited for; matrix products, arithmetic and copies ran while one was open for 6% of the time, Pallas kernels for 0%

commit v1 on v0

--- a/solution.py
+++ b/solution.py
@@ -1,7 +1,40 @@
+import functools
 import jax
 import jax.numpy as jnp
 from jax import lax
 from jax.sharding import PartitionSpec as P
+
+
+def set_ends(own_rows, which_dim, xx):
+    aux = own_rows.shape
+    front = own_rows.reshape(*aux[:which_dim], xx, aux[which_dim] // xx, *aux[which_dim + 1 :])
+    return jnp.moveaxis(front, which_dim, 0)
+
+
+def islands_state(load, row_dim):
+    frame_out = list(load.shape[1:])
+    frame_out[row_dim] *= load.shape[0]
+    return jnp.moveaxis(load, 0, row_dim).reshape(frame_out)
+
+
+def _note_groups(z, group_axis, piece_in, mine_x):
+    arr_now = lax.axis_size(group_axis)
+    t1 = lax.axis_index(group_axis)
+    next_value, e_next = (arr_now, t1)
+    y2 = set_ends(z, piece_in, next_value)
+    column = [y2[e_next]]
+    for it in tuple(range(1, next_value)):
+        state_now = y2[(e_next + it) % next_value]
+        parts_out = lax.ppermute(
+            state_now, group_axis, [(idx, (idx + it) % next_value) for idx in range(next_value)]
+        )
+        column.append(parts_out)
+    small = jnp.stack(column)
+    y2 = small[(e_next - jnp.arange(next_value)) % next_value]
+    return islands_state(y2, mine_x)
+
+
+fit_copies = functools.partial(_note_groups, group_axis="conv", piece_in=1, mine_x=1)
 
 
 def padded(cells, sides, width):
@@ -78,11 +111,7 @@
     )
     outgoing = jnp.dot(subgrid, placement, preferred_element_type=jnp.float32).astype(jnp.bfloat16)
     incoming = lax.all_to_all(
-        convolve(
-            lax.all_to_all(outgoing, "conv", split_axis=1, concat_axis=1, tiled=True),
-            conv_blocks,
-            band_shift,
-        ),
+        convolve(fit_copies(outgoing), conv_blocks, band_shift),
         "conv",
         split_axis=1,
         concat_axis=1,

time: 51.4 us -> 47.6 us (0.926)
  starting transfers between devices: 15.3 us -> 12.6 us
  waiting for transfers between devices: 7.66 us -> 6.01 us
    all_to_all x1 -> x0, waiting for transfers between devices: 5.95 us -> none  [on_device(): lax.all_to_all(outgoing, 'conv', split_axis=1, concat_axis=1, tiled=True)]
    ppermute x0 -> x3, waiting for transfers between devices: none -> 4.34 us  [_note_groups(): lax.ppermute(state_now, group_axis, [(idx, (idx + it) % next_value) for i...]
    all_to_all x1 -> x0, starting transfers between devices: 3.41 us -> none  [on_device(): lax.all_to_all(outgoing, 'conv', split_axis=1, concat_axis=1, tiled=True)]
    all_to_all x3 -> x1, local copies, waits for them, and re-layouts: 1.1 us -> 0.14 us  [on_device(): lax.all_to_all(convolve(fit_copies(outgoing), conv_blocks, band_shift), '...]
    another operation x0 -> x2, local copies, waits for them, and re-layouts: none -> 0.73 us
    ppermute x0 -> x3, starting transfers between devices: none -> 0.7 us  [_note_groups(): lax.ppermute(state_now, group_axis, [(idx, (idx + it) % next_value) for i...]
    gather x0 -> x1, local copies, waits for them, and re-layouts: none -> 0.6 us  [_note_groups(): y2 = small[(e_next - jnp.arange(next_value)) % next_value]]
    unnamed x9 -> x13, local copies, waits for them, and re-layouts: 1.32 us -> 1.37 us
  transfers between devices with their start and end apart: 5 -> 7, of which waited for: 3 -> 4; matrix products, arithmetic and copies ran while one was open for 6% -> 7% of each run, Pallas kernels for 0% -> 0%
where the time goes in v1:
time: 47.6 us; the launch traced here: 47.4 us
  starting transfers between devices  12.6 us (26%)
  blocking collectives  8.39 us (18%)
  matrix products  7.44 us (16%)
  local copies, waits for them, and re-layouts  6.84 us (14%)
  waiting for transfers between devices  6.01 us (13%)
  other arithmetic  5.77 us (12%)
    ppermute x2, starting transfers between devices, padded(): lax.ppermute(head, axis, [((i + 1) % count, i) for i in range(count)])  11.3 us
    all_to_all x1, blocking collectives, on_device(): lax.all_to_all(convolve(fit_copies(outgoing), conv_blocks, band_shift), '...  8.39 us
    ppermute x3, waiting for transfers between devices, _note_groups(): lax.ppermute(state_now, group_axis, [(idx, (idx + it) % next_value) for i...  4.34 us
    dot_general x1, matrix products, convolve(): jnp.einsum('rjbp,jbs->rsp', backward, select.astype(jnp.float32), precisi...  2.94 us
    dot_general x1, matrix products, convolve(): jnp.einsum('rjq,jbpq->rjbp', forward, conv_blocks, preferred_element_type...  2.02 us
    ppermute x2, waiting for transfers between devices, padded(): lax.ppermute(tail, axis, [(i, (i + 1) % count) for i in range(count)])  1.61 us
    scatter-add x1, other arithmetic, on_device(): result = interior_part.at[:, left_list].add(edge_sums[:, :rim_width])  1.59 us
    scatter-add x1, other arithmetic, on_device(): result = result.at[:, right_list].add(edge_sums[:, 3 * rim_width:])  1.59 us
  transfers between devices with their start and end apart: 7, of which 4 were waited for; matrix products, arithmetic and copies ran while one was open for 7% of the time, Pallas kernels for 0%

profile of v1, /device:TPU:0, one launch (start us, length us, event | category | flops | bytes accessed | tf_op | source)
XLA Modules:
  0.0 47.4 jit_solution(10253065926290474254)
XLA Ops:
  0.0 0.0 copy-start
  0.0 0.0 copy-start.1
  0.0 0.0 copy-start.3
  0.0 0.8 %compare_and_fusion.1 = (pred[128]{0:T(512)(128)(4,1)S(1)}, s32[128]{0:T(128)S(1)}, pred[128]{0:T(512)(128)(4,1)S(1)}, s32[128]{0:T(128)S(1)}) fusion(s32[2,128]{1,0:T(2,128)} %param.13), kind=kLoop, calls=%fused_computation.67 | loop fusion | flops 1536 | bytes 2304 | tf_op jit(solution)/shard_map/jit(_take)/and | solution.py:96
  0.8 1.3 %copy.36 = bf16[256,768]{0,1:T(8,128)(2,1)S(1)} copy(f32[256,768]{1,0:T(8,128)} %param.8) | data formatting | bytes 1179648 | tf_op args[0]
  2.1 0.8 %gather_fusion.1 = bf16[128,256]{1,0:T(8,128)(2,1)S(1)} fusion(bf16[256,768]{0,1:T(8,128)(2,1)S(1)} %copy.36, s32[1024]{0:T(1024)S(1)} %pad_clamp_fusion.2), kind=kCustom, calls=%fused_computation.clone | custom fusion | bytes 131584 | tf_op jit(solution)/shard_map/jit(_take)/gather | solution.py:96
  2.9 0.1 select_bitcast_fusion.1
  3.0 0.6 %collective-permute-start = (bf16[256,128]{0,1:T(8,128)(2,1)S(1)}, bf16[256,128]{0,1:T(8,128)(2,1)S(1)}, u32[]{:S(2)}, u32[]{:S(2)}) collective-permute-start(bf16[256,128]{0,1:T(8,128)(2,1)S(1)} %select_bitcast_fusion.1), channel_id=1, source_target_pairs={{0,1},{1,2},{2,3},{3,4},{4,5},{5,6},{6,7},{7,8},{8,9},{9,10},{10,1... | collective-permute-start | bytes 196616 | tf_op jit(solution)/shard_map/ppermute | solution.py:47
  3.6 0.8 %gather_fusion.2 = bf16[128,256]{1,0:T(8,128)(2,1)S(1)} fusion(bf16[256,768]{0,1:T(8,128)(2,1)S(1)} %copy.36, s32[1024]{0:T(1024)S(1)} %pad_clamp_fusion.1), kind=kCustom, calls=%fused_computation.1.clone | custom fusion | bytes 131584 | tf_op jit(solution)/shard_map/jit(_take)/gather | solution.py:96
  4.4 0.1 select_bitcast_fusion
  4.5 6.0 %collective-permute-start.1 = (bf16[256,128]{0,1:T(8,128)(2,1)S(1)}, bf16[256,128]{0,1:T(8,128)(2,1)S(1)}, u32[]{:S(2)}, u32[]{:S(2)}) collective-permute-start(bf16[256,128]{0,1:T(8,128)(2,1)S(1)} %select_bitcast_fusion), channel_id=1, source_target_pairs={{1,0},{2,1},{3,2},{4,3},{5,4},{6,5},{7,6},{8,7},{9,8},{10,9},{11,1... | collective-permute-start | bytes 196616 | tf_op jit(solution)/shard_map/ppermute | solution.py:49
  10.5 0.0 copy-done.1
  10.6 1.2 %reduce-window.6 = s32[4,3,128]{2,1,0:T(4,128)S(1)} reduce-window(s32[4,3,128]{2,1,0:T(4,128)S(1)} %fusion.32, s32[]{:T(128)} %constant.63.clone.1), window={size=1x1x128 pad=0_0x0_0x127_0}, to_apply=%region_0.0 | reduce-window | flops 195072 | bytes 12292 | tf_op jit(solution)/shard_map/reduce-window
  11.8 0.2 slice_reduce_fusion
  12.0 0.2 reduce-window.9
  12.2 0.1 add_bitcast_fusion
  12.3 0.0 copy-done.3
  12.4 0.0 collective-permute-done
  12.4 0.1 collective-permute-done.1
  12.4 0.0 copy-done
  12.4 0.7 %convolution_convert_fusion.1 = bf16[256,512]{1,0:T(8,128)(2,1)S(1)} fusion(bf16[1024,384]{1,0:T(8,128)(2,1)S(1)} %copy-done, bf16[256,128]{0,1:T(8,128)(2,1)S(1)} %collective-permute-done.1, bf16[256,768]{0,1:T(8,128)(2,1)S(1)} %copy.36, bf16[256,128]{0,1:T(8,128)(2,1)S(1)} %collective-permute-done, s32[384]{0:T(512)S(1)} %add_reduce_fusion), kind=kOutput, calls=%fused_computation.12 | convolution fusion | flops 303988736 | bytes 1574400 | tf_op jit(solution)/shard_map/dot_general | solution.py:112
  13.1 0.1 reshape.144
  13.2 0.6 %constant_dynamic-slice_fusion.3 = (bf16[256,1,128]{2,1,0:T(2,128)(2,1)S(1)}, bf16[256,1,128]{2,1,0:T(2,128)(2,1)S(1)}, bf16[256,1,128]{2,1,0:T(2,128)(2,1)S(1)}, bf16[256,1,128]{2,1,0:T(2,128)(2,1)S(1)}) fusion(bf16[256,4,128]{2,1,0:T(4,128)(2,1)S(1)} %reshape.144, s32[]{:T(128)S(6)} %select_n.84, s32[]{:T(128)S(6)} %select_n.88, s32[]{:T(128)S(6)} %select_n.86, ...), kind=kLoop, calls=%fused_computation.77 | loop fusion | bytes 524304 | tf_op jit(solution)/shard_map/dynamic-slice
  13.8 0.1 collective-permute-start.3
  13.9 0.6 %collective-permute-start.4 = (bf16[256,128]{1,0:T(8,128)(2,1)S(1)}, bf16[256,128]{1,0:T(8,128)(2,1)S(1)}, u32[]{:S(2)}, u32[]{:S(2)}) collective-permute-start(bf16[256,128]{1,0:T(8,128)(2,1)S(1)} %bitcast.112), channel_id=1, source_target_pairs={{0,3},{1,0},{2,1},{3,2},{4,7},{5,4},{6,5},{7,6},{8,11},{9,8},{10,9... | collective-permute-start | bytes 196616 | tf_op jit(solution)/shard_map/ppermute | solution.py:28
  14.5 0.1 collective-permute-start.2
  14.6 4.2 %collective-permute-done.3 = bf16[256,128]{1,0:T(8,128)(2,1)S(1)} collective-permute-done((bf16[256,128]{1,0:T(8,128)(2,1)S(1)}, bf16[256,128]{1,0:T(8,128)(2,1)S(1)}, u32[]{:S(2)}, u32[]{:S(2)}) %collective-permute-start.3) | collective-permute-done | bytes 65568 | tf_op jit(solution)/shard_map/ppermute | solution.py:28
  18.7 0.0 collective-permute-done.4
  18.7 0.2 collective-permute-done.2
  18.9 0.6 %gather_fusion = bf16[4,256,128]{2,1,0:T(8,128)(2,1)S(1)} fusion(bf16[4,256,128]{2,1,0:T(8,128)(2,1)S(1)} %pad_maximum_fusion, s32[1024]{0:T(1024)S(1)} %pad_clamp_fusion), kind=kCustom, calls=%fused_computation.2 | custom fusion | bytes 524304 | tf_op jit(solution)/shard_map/gather | solution.py:33
  19.5 0.1 copy.41
  19.7 0.2 copy.42
  19.9 1.0 %fusion.2 = bf16[256,2,3,256]{3,2,0,1:T(4,128)(2,1)S(1)} fusion(bf16[256,2,256]{2,1,0:T(2,128)(2,1)S(1)} %copy.42, s32[2,3]{1,0:T(2,128)S(1)} %and_select_fusion.1), kind=kOutput, calls=%fused_computation.9 | convolution fusion | flops 1966092 | bytes 1048600 | tf_op jit(solution)/shard_map/rsp,jbs->rjbp/dot_general | solution.py:71
  20.9 2.0 %convolution_bitcast_fusion = f32[256,2,3,256]{3,0,2,1:T(8,128)S(1)} fusion(bf16[2,3,256,256]{3,2,1,0:T(8,128)(2,1)} %param.10, bf16[256,2,3,256]{3,2,0,1:T(4,128)(2,1)S(1)} %fusion.2), kind=kOutput, calls=%fused_computation.7 | convolution fusion | flops 402784256 | bytes 3145728 | tf_op jit(solution)/shard_map/rjq,jbpq->rjbp/dot_general | solution.py:77
  22.9 2.9 %fusion.10 = bf16[256,2,256]{2,1,0:T(2,128)(2,1)S(1)} fusion(f32[256,2,3,256]{3,0,2,1:T(8,128)S(1)} %convolution_bitcast_fusion, s32[2,3]{1,0:T(2,128)S(1)} %and_select_fusion.1), kind=kOutput, calls=%fused_computation.17 | convolution fusion | flops 9568268 | bytes 1835032 | tf_op jit(solution)/shard_map/rjbp,jbs->rsp/dot_general | solution.py:80
  25.9 0.2 convert_element_type.59
  26.1 8.4 %all_to_all.9 = bf16[256,4,128]{2,0,1:T(8,128)(2,1)S(1)} all-to-all(bf16[256,4,128]{2,0,1:T(8,128)(2,1)S(1)} %copy.45), channel_id=1, replica_groups=mesh['tile'=8,'conv'=4] {'conv'}, dimensions={1} | all-to-all | bytes 524288 | tf_op jit(solution)/shard_map/all_to_all | solution.py:113
  34.5 0.1 copy.46
  34.6 0.0 copy-start.2
  34.6 0.8 %fusion.48 = (bf16[256,1024]{1,0:T(8,128)(2,1)S(1)}, f32[256,1024]{1,0:T(8,128)S(1)}) fusion(bf16[1024,384]{1,0:T(8,128)(2,1)S(1)} %copy-done, bf16[256,512]{0,1:T(8,128)(2,1)S(1)} %bitcast.107, s32[384]{0:T(512)S(1)} %add_reduce_fusion), kind=kOutput, calls=%fused_computation.84 | convolution fusion | flops 302546944 | bytes 2622976 | tf_op jit(solution)/shard_map/dot_general | solution.py:57
  35.5 0.1 collective-permute-start.5
  35.5 5.3 %collective-permute-start.6 = (bf16[256,128]{1,0:T(8,128)(2,1)S(1)}, bf16[256,128]{1,0:T(8,128)(2,1)S(1)}, u32[]{:S(2)}, u32[]{:S(2)}) collective-permute-start(bf16[256,128]{1,0:T(8,128)(2,1)S(1)} %get-tuple-element.11), channel_id=1, source_target_pairs={{1,0},{2,1},{3,2},{4,3},{5,4},{6,5},{7,6},{8,7},{9,8},{10,9},{11,1... | collective-permute-start | bytes 196616 | tf_op jit(solution)/shard_map/ppermute | solution.py:49
  40.8 0.0 copy-done.2
  40.9 0.1 slice.47
  40.9 0.3 copy.47
  41.2 1.6 %collective-permute-done.5 = bf16[256,128]{1,0:T(8,128)(2,1)S(1)} collective-permute-done((bf16[256,128]{1,0:T(8,128)(2,1)S(1)}, bf16[256,128]{1,0:T(8,128)(2,1)S(1)}, u32[]{:S(2)}, u32[]{:S(2)}) %collective-permute-start.5) | collective-permute-done | bytes 65568 | tf_op jit(solution)/shard_map/ppermute | solution.py:47
  42.8 0.0 collective-permute-done.6
  42.8 0.1 copy.48
  42.9 0.1 copy.49
  43.0 1.6 %scatter_fusion = f32[256,768]{0,1:T(8,128)S(1)} fusion(f32[256,768]{0,1:T(8,128)S(1)} %copy.47, s32[128]{0:T(128)S(1)} %get-tuple-element.19, f32[128,256]{1,0:T(8,128)S(1)} %copy.48), kind=kCustom, calls=%fused_computation.3 | custom fusion | flops 32768 | bytes 393728 | tf_op jit(solution)/shard_map/scatter-add | solution.py:130
  44.6 1.6 %scatter_fusion.1 = f32[256,768]{0,1:T(8,128)S(1)} fusion(f32[256,768]{0,1:T(8,128)S(1)} %scatter_fusion, s32[128]{0:T(128)S(1)} %get-tuple-element.18, f32[128,256]{1,0:T(8,128)S(1)} %copy.49), kind=kCustom, calls=%fused_computation.4 | custom fusion | flops 32768 | bytes 393728 | tf_op jit(solution)/shard_map/scatter-add | solution.py:131
  46.2 1.1 %copy.50 = f32[256,768]{1,0:T(8,128)} copy(f32[256,768]{0,1:T(8,128)S(1)} %scatter_fusion.1) | data formatting | bytes 1572864 | tf_op jit(solution)/shard_map/scatter-add | solution.py:131
  (18 shorter events, 0.3 us)
Async XLA Ops:
  0.0 12.4 %copy-start = (bf16[1024,384]{1,0:T(8,128)(2,1)S(1)}, bf16[1024,384]{1,0:T(8,128)(2,1)}, u32[]{:S(2)}) copy-start(bf16[1024,384]{1,0:T(8,128)(2,1)} %param.9) | copy-start | bytes 2359300
  0.0 10.5 %copy-start.1 = (s32[384,1]{0,1:T(1,128)S(1)}, s32[384,1]{0,1:T(1,128)}, u32[]{:S(2)}) copy-start(s32[384,1]{0,1:T(1,128)} %param.12) | copy-start | bytes 4612
  0.0 12.3 %copy-start.3 = (s32[2,3]{1,0:T(2,128)S(1)}, s32[2,3]{1,0:T(2,128)}, u32[]{:S(2)}) copy-start(s32[2,3]{1,0:T(2,128)} %param.11) | copy-start | bytes 76
  3.0 9.3 %collective-permute-start = (bf16[256,128]{0,1:T(8,128)(2,1)S(1)}, bf16[256,128]{0,1:T(8,128)(2,1)S(1)}, u32[]{:S(2)}, u32[]{:S(2)}) collective-permute-start(bf16[256,128]{0,1:T(8,128)(2,1)S(1)} %select_bitcast_fusion.1), channel_id=1, source_target_pairs={{0,1},{1,2},{2,3},{3,4},{4,5},{5,6},{6,7},{7,8},{8,9},{9,10},{10,1... | collective-permute-start | bytes 196616 | tf_op jit(solution)/shard_map/ppermute | solution.py:47
  4.5 7.9 %collective-permute-start.1 = (bf16[256,128]{0,1:T(8,128)(2,1)S(1)}, bf16[256,128]{0,1:T(8,128)(2,1)S(1)}, u32[]{:S(2)}, u32[]{:S(2)}) collective-permute-start(bf16[256,128]{0,1:T(8,128)(2,1)S(1)} %select_bitcast_fusion), channel_id=1, source_target_pairs={{1,0},{2,1},{3,2},{4,3},{5,4},{6,5},{7,6},{8,7},{9,8},{10,9},{11,1... | collective-permute-start | bytes 196616 | tf_op jit(solution)/shard_map/ppermute | solution.py:49
  13.8 5.0 %collective-permute-start.3 = (bf16[256,128]{1,0:T(8,128)(2,1)S(1)}, bf16[256,128]{1,0:T(8,128)(2,1)S(1)}, u32[]{:S(2)}, u32[]{:S(2)}) collective-permute-start(bf16[256,128]{1,0:T(8,128)(2,1)S(1)} %bitcast.111), channel_id=1, source_target_pairs={{0,2},{1,3},{2,0},{3,1},{4,6},{5,7},{6,4},{7,5},{8,10},{9,11},{10,... | collective-permute-start | bytes 196616 | tf_op jit(solution)/shard_map/ppermute | solution.py:28
  13.9 4.9 %collective-permute-start.4 = (bf16[256,128]{1,0:T(8,128)(2,1)S(1)}, bf16[256,128]{1,0:T(8,128)(2,1)S(1)}, u32[]{:S(2)}, u32[]{:S(2)}) collective-permute-start(bf16[256,128]{1,0:T(8,128)(2,1)S(1)} %bitcast.112), channel_id=1, source_target_pairs={{0,3},{1,0},{2,1},{3,2},{4,7},{5,4},{6,5},{7,6},{8,11},{9,8},{10,9... | collective-permute-start | bytes 196616 | tf_op jit(solution)/shard_map/ppermute | solution.py:28
  14.5 4.4 %collective-permute-start.2 = (bf16[256,128]{1,0:T(8,128)(2,1)S(1)}, bf16[256,128]{1,0:T(8,128)(2,1)S(1)}, u32[]{:S(2)}, u32[]{:S(2)}) collective-permute-start(bf16[256,128]{1,0:T(8,128)(2,1)S(1)} %bitcast.113), channel_id=1, source_target_pairs={{0,1},{1,2},{2,3},{3,0},{4,5},{5,6},{6,7},{7,4},{8,9},{9,10},{10,1... | collective-permute-start | bytes 196616 | tf_op jit(solution)/shard_map/ppermute | solution.py:28
  34.6 6.2 %copy-start.2 = (s32[2,128]{1,0:T(2,128)S(1)}, s32[2,128]{1,0:T(2,128)}, u32[]{:S(2)}) copy-start(s32[2,128]{1,0:T(2,128)} %param.13) | copy-start | bytes 3076
  35.5 7.3 %collective-permute-start.5 = (bf16[256,128]{1,0:T(8,128)(2,1)S(1)}, bf16[256,128]{1,0:T(8,128)(2,1)S(1)}, u32[]{:S(2)}, u32[]{:S(2)}) collective-permute-start(bf16[256,128]{1,0:T(8,128)(2,1)S(1)} %get-tuple-element.10), channel_id=1, source_target_pairs={{0,1},{1,2},{2,3},{3,4},{4,5},{5,6},{6,7},{7,8},{8,9},{9,10},{10,1... | collective-permute-start | bytes 196616 | tf_op jit(solution)/shard_map/ppermute | solution.py:47
  35.5 7.3 %collective-permute-start.6 = (bf16[256,128]{1,0:T(8,128)(2,1)S(1)}, bf16[256,128]{1,0:T(8,128)(2,1)S(1)}, u32[]{:S(2)}, u32[]{:S(2)}) collective-permute-start(bf16[256,128]{1,0:T(8,128)(2,1)S(1)} %get-tuple-element.11), channel_id=1, source_target_pairs={{1,0},{2,1},{3,2},{4,3},{5,4},{6,5},{7,6},{8,7},{9,8},{10,9},{11,1... | collective-permute-start | bytes 196616 | tf_op jit(solution)/shard_map/ppermute | solution.py:49
